TPU v7x, 32 devices: a whole 2x2x4 slice. The times are simulated.
32 devices in a mesh: chip: 2 (over y), board: 4 (over z), cuts: 4 (over x, core).
Axes of the slice: x: 2, y: 2, z: 4, core: 2. Of those that a mesh axis runs over, the one named last changes fastest.
Arguments:
- features: bfloat16 [32, 2048, 1024], P(('chip', 'board', 'cuts')), may hold values from -6 to 6
- targets: bfloat16 [32, 2048, 256], P(('chip', 'board', 'cuts')), may hold values from -24 to 24
- lower_weight: bfloat16 [32, 1024, 512], P(('chip', 'board', 'cuts')), may hold values from -0.1875 to 0.1875
- head_weight: float32 [32, 512, 256], P(('chip', 'board', 'cuts')), may hold values from -0.25 to 0.25
- batch_rows: int32 [32, 2, 1024], P(('chip', 'board', 'cuts')), may hold values from 0 to 2047
- sample_counts: int32 [32], P(('chip', 'board', 'cuts')), may hold values from 1 to 1000
- cluster_ids: int32 [32], P(('chip', 'board', 'cuts')), may hold values from 0 to 7, as said below
Outputs:
- cluster_step: float32 [32, 512, 256], P(('chip', 'board', 'cuts'))
Inputs may be any that keep to these rules, and one draw needn't show every extreme that they name: `cluster_ids`: every one of the 8 clusters has at least one client.
All inputs are finite; a program needn't handle non-finite values.
Results may differ from a plain program's by a relative error of at most 0.0003.
Values sent between devices are 32-bit elements; how exact they have to be, the bound alone decides.
No kernel may reach another device: no remote copies, remote signals or barrier semaphores. Data moves between devices by JAX's collectives and lax.ppermute only.
A program may use at most 64 MiB of HBM per device.

v0:
```python
import jax
import jax.numpy as jnp
from jax import lax
from jax.sharding import PartitionSpec as P

LR = 0.5


def on_device(features, targets, lower_weight, head_weight, batch_rows, sample_counts, cluster_ids):
    hidden = jnp.tanh(jnp.dot(features[0], lower_weight[0], preferred_element_type=jnp.float32))
    start = head_weight[0]
    weight = start
    count_rows = batch_rows.shape[2]
    for step in range(batch_rows.shape[1]):
        picked = jnp.take(hidden, batch_rows[0, step], axis=0)
        wanted = jnp.take(targets[0], batch_rows[0, step], axis=0).astype(jnp.float32)
        err = jnp.dot(picked, weight, precision=lax.Precision.HIGHEST) - wanted
        grad = jnp.dot(picked.T, err, precision=lax.Precision.HIGHEST) / count_rows
        weight = weight - LR * grad
    delta = weight - start
    cluster = cluster_ids[0]
    number = 8
    chip_count = lax.axis_size("chip")
    rest_count = lax.axis_size(("board", "cuts"))
    every_id, every_count = (
        lax.all_gather(cluster_ids, ("chip", "board", "cuts"), axis=0, tiled=True),
        lax.all_gather(sample_counts, ("chip", "board", "cuts"), axis=0, tiled=True),
    )
    table = (every_id[:, None] == jnp.arange(number, dtype=jnp.int32)[None, :]).astype(jnp.float32)
    weighted = table * every_count.astype(jnp.float32)[:, None]
    counts = jnp.sum(weighted, axis=0)
    scaled = (sample_counts[0].astype(jnp.float32) * delta).reshape(chip_count, rest_count, -1)
    columns = lax.all_to_all(
        lax.all_to_all(scaled, "chip", split_axis=0, concat_axis=0, tiled=True),
        ("board", "cuts"),
        split_axis=1,
        concat_axis=1,
        tiled=True,
    )
    columns = columns.reshape(chip_count * rest_count, -1)
    share = jnp.dot(table.T, columns, precision=lax.Precision.HIGHEST)
    outgoing = jnp.dot(table, share, precision=lax.Precision.HIGHEST)
    outgoing = outgoing.reshape(chip_count, rest_count, -1)
    arrived = lax.all_to_all(
        lax.all_to_all(outgoing, "chip", split_axis=0, concat_axis=0, tiled=True),
        ("board", "cuts"),
        split_axis=1,
        concat_axis=1,
        tiled=True,
    )
    mine = arrived.reshape(delta.shape)
    denom = lax.dynamic_index_in_dim(counts, cluster, 0, keepdims=False)
    return (mine / (LR * denom))[None]


def solution(mesh):
    return jax.shard_map(
        on_device,
        mesh=mesh,
        in_specs=(
            P(("chip", "board", "cuts"), None, None),
            P(("chip", "board", "cuts"), None, None),
            P(("chip", "board", "cuts"), None, None),
            P(("chip", "board", "cuts"), None, None),
            P(("chip", "board", "cuts"), None, None),
            P(("chip", "board", "cuts")),
            P(("chip", "board", "cuts")),
        ),
        out_specs=P(("chip", "board", "cuts"), None, None),
        check_vma=False,
    )
```

profile of v0, /device:TPU:0, one launch (start us, length us, event | category | flops | bytes accessed | tf_op | source)
XLA Modules:
  0.0 138.6 jit_solution(8541357281149164295)
XLA Ops:
  0.0 0.0 copy-start
  0.0 0.8 fusion.57
  0.8 0.4 copy-done
  1.3 6.5 %fusion.2 = f32[2048,512]{1,0:T(8,128)} fusion(bf16[1,2048,1024]{2,1,0:T(8,128)(2,1)} %param.11, bf16[1,1024,512]{2,1,0:T(8,128)(2,1)S(1)} %copy-done), kind=kOutput, calls=%fused_computation.6 | convolution fusion | flops 2147483648 | bytes 9437184 | tf_op jit(solution)/shard_map/dot_general | solution.py:10
  7.7 7.5 %gather_fusion = f32[1024,512]{1,0:T(8,128)} fusion(f32[2048,512]{1,0:T(8,128)} %fusion.2, s32[1024]{0:T(1024)S(1)} %fusion.49), kind=kCustom, calls=%fused_computation.clone | custom fusion | bytes 4198400 | tf_op jit(solution)/shard_map/jit(_take)/gather | solution.py:15
  15.3 0.0 copy-done.1
  15.3 5.0 %gather_fusion.1 = bf16[1024,256]{1,0:T(8,128)(2,1)} fusion(bf16[2048,256]{1,0:T(8,128)(2,1)S(1)} %bitcast.29, s32[1024]{0:T(1024)S(1)} %fusion.49), kind=kCustom, calls=%fused_computation.1.clone | custom fusion | bytes 1052672 | tf_op jit(solution)/shard_map/jit(_take)/gather | solution.py:16
  20.2 7.5 %gather_fusion.2 = f32[1024,512]{1,0:T(8,128)} fusion(f32[2048,512]{1,0:T(8,128)} %fusion.2, s32[1024]{0:T(1024)S(1)} %fusion.50), kind=kCustom, calls=%fused_computation.2.clone | custom fusion | bytes 4198400 | tf_op jit(solution)/shard_map/jit(_take)/gather | solution.py:15
  27.7 3.9 %gather_fusion.3 = bf16[1024,256]{1,0:T(8,128)(2,1)S(1)} fusion(bf16[2048,256]{1,0:T(8,128)(2,1)S(1)} %bitcast.30, s32[1024]{0:T(1024)S(1)} %fusion.50), kind=kCustom, calls=%fused_computation.3.clone | custom fusion | bytes 1052672 | tf_op jit(solution)/shard_map/jit(_take)/gather | solution.py:16
  31.7 3.7 %fusion.13 = f32[1024,256]{1,0:T(8,128)S(1)} fusion(f32[1024,512]{1,0:T(8,128)} %gather_fusion, pred[1024]{0:T(1024)(128)(4,1)S(1)} %compare_and_fusion.1, f32[1,512,256]{2,1,0:T(8,128)S(1)} %copy-done.4, bf16[1024,256]{1,0:T(8,128)(2,1)} %gather_fusion.1), kind=kOutput, calls=%fused_computation.15 | convolution fusion | flops 1611923456 | bytes 4195328 | tf_op jit(solution)/shard_map/dot_general | solution.py:17
  35.4 3.6 %fusion.34 = f32[512,256]{1,0:T(8,128)S(1)} fusion(f32[1024,256]{1,0:T(8,128)S(1)} %fusion.13, f32[1024,512]{1,0:T(8,128)S(1)} %copy-done.2, pred[1024]{0:T(1024)(128)(4,1)S(1)} %compare_and_fusion.1, f32[1,512,256]{2,1,0:T(8,128)S(1)} %copy-done.4), kind=kOutput, calls=%fused_computation.22 | convolution fusion | flops 1611399168 | bytes 4195328 | tf_op jit(solution)/shard_map/dot_general | solution.py:18
  39.7 2.4 %fusion.16 = f32[1024,256]{1,0:T(8,128)S(1)} fusion(f32[512,256]{1,0:T(8,128)S(1)} %fusion.34, f32[1024,512]{1,0:T(8,128)S(1)} %copy-done.3, pred[1024]{0:T(1024)(128)(4,1)S(1)} %compare_and_fusion, bf16[1024,256]{1,0:T(8,128)(2,1)S(1)} %gather_fusion.3), kind=kOutput, calls=%fused_computation.16 | convolution fusion | flops 1611923456 | bytes 4195328 | tf_op jit(solution)/shard_map/dot_general | solution.py:17
  42.1 3.6 %fusion.31 = f32[512,256]{1,0:T(8,128)S(1)} fusion(f32[512,256]{1,0:T(8,128)S(1)} %fusion.34, f32[1024,256]{1,0:T(8,128)S(1)} %fusion.16, f32[1024,512]{1,0:T(8,128)S(1)} %copy-done.3, pred[1024]{0:T(1024)(128)(4,1)S(1)} %compare_and_fusion, f32[1,512,256]{2,1,0:T(8,128)S(1)} %copy-done.4, f32[]{:T(128)} %bitcast), kind=kOutput, calls=%fused_computation.21 | convolution fusion | flops 1611661312 | bytes 4719620 | tf_op jit(solution)/shard_map/dot_general | solution.py:18
  45.8 0.1 reshape.37
  45.9 12.1 %all_to_all.20 = f32[2,16,4096]{2,1,0:T(8,128)S(1)} all-to-all(f32[2,16,4096]{2,1,0:T(8,128)S(1)} %reshape.37), channel_id=1, replica_groups=mesh['chip'=2,'board'=4,'cuts'=4] {'chip'}, dimensions={0} | all-to-all | bytes 1048576 | tf_op jit(solution)/shard_map/all_to_all | solution.py:34
  58.0 1.2 copy.22
  59.2 5.9 %all-to-all-start.1 = ((f32[2,16,4096]{2,0,1:T(2,128)}), f32[2,16,4096]{2,0,1:T(2,128)S(1)}, u32[]{:S(2)}, u32[]{:S(2)}) async-start(f32[2,16,4096]{2,0,1:T(2,128)} %copy.22), calls=%async_computation.1 | async-start | bytes 1048576 | tf_op jit(solution)/shard_map/all_to_all | solution.py:33
  65.8 0.1 dynamic-update-slice.1
  65.9 0.1 dynamic-update-slice
  66.0 40.0 %all-reduce.2 = (s32[32]{0:T(128)S(1)}, s32[32]{0:T(128)S(1)}) all-reduce(s32[32]{0:T(128)S(1)} %dynamic-update-slice, s32[32]{0:T(128)S(1)} %dynamic-update-slice.1), channel_id=1, replica_groups=mesh['chip'=2,'board'=4,'cuts'=4] {'chip','board','cuts'}, use_global_device_ids=true, to_apply=%add | all-reduce | flops 64 | bytes 512
  106.0 0.0 all-to-all-done.1
  106.0 0.3 copy.23
  106.3 0.3 fusion.48
  106.6 0.4 fusion.47
  107.0 10.5 %all_to_all.21 = f32[2,16,4096]{2,1,0:T(8,128)S(1)} all-to-all(f32[2,16,4096]{2,1,0:T(8,128)S(1)} %bitcast.32), channel_id=1, replica_groups=mesh['chip'=2,'board'=4,'cuts'=4] {'chip'}, dimensions={0} | all-to-all | bytes 1048576 | tf_op jit(solution)/shard_map/all_to_all | solution.py:45
  117.5 1.2 copy.24
  118.7 4.4 %all-to-all-start.3 = ((f32[2,16,4096]{2,0,1:T(2,128)}), f32[2,16,4096]{2,0,1:T(2,128)S(1)}, u32[]{:S(2)}, u32[]{:S(2)}) async-start(f32[2,16,4096]{2,0,1:T(2,128)} %copy.24), calls=%async_computation.3 | async-start | bytes 1048576 | tf_op jit(solution)/shard_map/all_to_all | solution.py:44
  123.2 0.1 select_reduce_fusion
  123.3 0.6 dynamic_slice.4
  124.4 13.0 %all-to-all-done.3 = f32[2,16,4096]{2,0,1:T(2,128)S(1)} async-done(((f32[2,16,4096]{2,0,1:T(2,128)}), f32[2,16,4096]{2,0,1:T(2,128)S(1)}, u32[]{:S(2)}, u32[]{:S(2)}) %all-to-all-start.3) | async-done | bytes 524320 | tf_op jit(solution)/shard_map/all_to_all | solution.py:44
  137.4 0.3 copy_divide_fusion
  137.7 0.9 div.20
  (14 shorter events, 0.0 us)
Async XLA Ops:
  0.0 1.3 copy-start
  7.7 7.5 %copy-start.1 = (bf16[1,2048,256]{2,1,0:T(8,128)(2,1)S(1)}, bf16[1,2048,256]{2,1,0:T(8,128)(2,1)}, u32[]{:S(2)}) copy-start(bf16[1,2048,256]{2,1,0:T(8,128)(2,1)} %param.12) | copy-start | bytes 3145732
  27.7 4.0 %copy-start.4 = (f32[1,512,256]{2,1,0:T(8,128)S(1)}, f32[1,512,256]{2,1,0:T(8,128)}, u32[]{:S(2)}) copy-start(f32[1,512,256]{2,1,0:T(8,128)} %param.14) | copy-start | bytes 1572868
  31.7 3.7 %copy-start.2 = (f32[1024,512]{1,0:T(8,128)S(1)}, f32[1024,512]{1,0:T(8,128)}, u32[]{:S(2)}) copy-start(f32[1024,512]{1,0:T(8,128)} %gather_fusion) | copy-start | bytes 6291460
  35.4 4.3 %copy-start.3 = (f32[1024,512]{1,0:T(8,128)S(1)}, f32[1024,512]{1,0:T(8,128)}, u32[]{:S(2)}) copy-start(f32[1024,512]{1,0:T(8,128)} %gather_fusion.2) | copy-start | bytes 6291460
  59.2 46.8 %all-to-all-start.1 = ((f32[2,16,4096]{2,0,1:T(2,128)}), f32[2,16,4096]{2,0,1:T(2,128)S(1)}, u32[]{:S(2)}, u32[]{:S(2)}) async-start(f32[2,16,4096]{2,0,1:T(2,128)} %copy.22), calls=%async_computation.1 | async-start | bytes 1048576 | tf_op jit(solution)/shard_map/all_to_all | solution.py:33
  118.7 18.7 %all-to-all-start.3 = ((f32[2,16,4096]{2,0,1:T(2,128)}), f32[2,16,4096]{2,0,1:T(2,128)S(1)}, u32[]{:S(2)}, u32[]{:S(2)}) async-start(f32[2,16,4096]{2,0,1:T(2,128)} %copy.24), calls=%async_computation.3 | async-start | bytes 1048576 | tf_op jit(solution)/shard_map/all_to_all | solution.py:44
where the time goes:
time: 139 us
  blocking collectives  62.6 us (45%)
  local copies, waits for them, and re-layouts  29.7 us (21%)
  matrix products  20.5 us (15%)
  waiting for transfers between devices  13 us (9%)
  starting transfers between devices  10.4 us (7%)
  between operations  2.04 us (1%)
    unnamed x1, blocking collectives  40 us
    gather x2, local copies, waits for them, and re-layouts, on_device(): picked = jnp.take(hidden, batch_rows[0, step], axis=0)  15 us
    all_to_all x1, waiting for transfers between devices, on_device(): lax.all_to_all(lax.all_to_all(outgoing, 'chip', split_axis=0, concat_axis...  13 us
    all_to_all x1, blocking collectives, on_device(): lax.all_to_all(scaled, 'chip', split_axis=0, concat_axis=0, tiled=True)  12.1 us
    all_to_all x1, blocking collectives, on_device(): lax.all_to_all(outgoing, 'chip', split_axis=0, concat_axis=0, tiled=True)  10.5 us
    gather x2, local copies, waits for them, and re-layouts, on_device(): jnp.take(targets[0], batch_rows[0, step], axis=0).astype(jnp.float32)  8.91 us
    dot_general x2, matrix products, on_device(): grad = jnp.dot(picked.T, err, precision=lax.Precision.HIGHEST) / count_rows  7.26 us
    dot_general x1, matrix products, on_device(): jnp.dot(features[0], lower_weight[0], preferred_element_type=jnp.float32)  6.46 us
  transfers between devices with their start and end apart: 2, of which 1 were waited for; matrix products, arithmetic and copies ran while one was open for 1% of the time, Pallas kernels for 0%

commit v1 on v0

v1 whole, which is shorter than its diff:
```python
import functools

import jax
import jax.numpy as jnp
from jax import lax
from jax.experimental import pallas as pl
from jax.experimental.pallas import tpu as pltpu
from jax.sharding import PartitionSpec as P

LR = 0.5
CLUSTERS = 8
LANES = 128
SUB = 8
AXES = ("chip", "board", "cuts")
F32 = jnp.float32
BF16 = jnp.bfloat16


def halves(value):
    high = value.astype(BF16)
    return high, (value - high.astype(F32)).astype(BF16)


def product(a, b, contract):
    dims = (contract, ((), ()))
    dot = functools.partial(lax.dot_general, dimension_numbers=dims, preferred_element_type=F32)
    return dot(a[0], b[0]) + (dot(a[0], b[1]) + dot(a[1], b[0]))


def client_kernel(
    rows_ref, count_ref, cluster_ref, features_ref, lower_ref, targets_ref, head_ref, out_ref,
    feat, low, targ, start, pool, picked, grad, weight, arrived, *, shares, chunk,
):
    pool_rows, hidden = feat.shape[0], low.shape[1]
    steps, count_rows = rows_ref.shape
    outs = targ.shape[1]
    blocks, tblocks = hidden // LANES, outs // LANES

    def part(i):
        at = pl.ds(i * chunk, chunk)
        return pltpu.make_async_copy(features_ref.at[0, at], feat.at[at], arrived.at[i])

    chunks = pool_rows // chunk
    whole = [
        pltpu.make_async_copy(lower_ref.at[0], low, arrived.at[chunks]),
        pltpu.make_async_copy(targets_ref.at[0], targ, arrived.at[chunks + 1]),
        pltpu.make_async_copy(head_ref.at[0], start, arrived.at[chunks + 2]),
    ]
    whole[0].start()
    for i in range(chunks):
        part(i).start()
    whole[1].start()
    whole[2].start()
    whole[0].wait()
    whole[1].wait()

    @pl.loop(0, chunks)
    def _(i):
        part(i).wait()
        at = pl.ds(pl.multiple_of(i * chunk, chunk), chunk)
        h = jnp.tanh(jnp.dot(feat[at, :], low[...], preferred_element_type=F32))
        t = targ[at, :].astype(F32)
        for k in range(blocks):
            pool[pl.ds(i * chunk * SUB + k, chunk, stride=SUB), :] = h[:, k * LANES:(k + 1) * LANES]
        for k in range(tblocks):
            pool[pl.ds(i * chunk * SUB + blocks + k, chunk, stride=SUB), :] = t[:, k * LANES:(k + 1) * LANES]

    whole[2].wait()
    total = steps * (count_rows // chunk)

    def gather(slot, i):
        step, at = i // (count_rows // chunk), (i % (count_rows // chunk)) * chunk
        for r in range(chunk):
            row = rows_ref[step, at + r]
            picked[slot, r * SUB:(r + 1) * SUB, :] = pool[pl.ds(pl.multiple_of(row * SUB, SUB), SUB), :]

    def one(slot):
        view = picked.at[slot]
        h = halves(jnp.concatenate([view[pl.ds(k, chunk, stride=SUB), :] for k in range(blocks)], axis=1))
        t = jnp.concatenate([view[pl.ds(blocks + k, chunk, stride=SUB), :] for k in range(tblocks)], axis=1)
        err = product(h, (weight[0], weight[1]), ((1,), (0,))) - t
        grad[...] += product(h, halves(err), ((0,), (0,)))

    def load_weight(value):
        high, rest = halves(value)
        weight[0], weight[1] = high, rest

    load_weight(start[...])
    grad[...] = jnp.zeros_like(grad)
    gather(0, 0)
    per_step = count_rows // chunk
    for step in range(steps):
        @pl.loop(0, per_step // 2)
        def _(j):
            i = step * per_step + 2 * j
            gather(1, i + 1)
            one(0)
            gather(0, jnp.minimum(i + 2, total - 1))
            one(1)
        if step + 1 < steps:
            load_weight(start[...] - (LR / count_rows) * grad[...])

    each = hidden // shares
    width = tblocks * each + 1
    count = count_ref[0].astype(F32)
    scale = -(LR / count_rows)
    lane = lax.broadcasted_iota(jnp.int32, (1, LANES), 1)
    note = jnp.where(lane < LANES // 2, cluster_ref[0].astype(F32), count)
    for s in range(shares):
        for k in range(tblocks):
            out_ref[s * width + k * each:s * width + (k + 1) * each, :] = (
                grad[s * each:(s + 1) * each, k * LANES:(k + 1) * LANES] * scale
            )
        out_ref[(s + 1) * width - 1:(s + 1) * width, :] = note


def cluster_kernel(in_ref, out_ref, *, shares):
    each, outs = out_ref.shape[1], out_ref.shape[2]
    tblocks = outs // LANES
    data = tblocks * each
    width = data + 1
    full = (data, LANES)
    sums = [jnp.zeros(full, F32)] * CLUSTERS
    counts = [jnp.zeros((1, LANES), F32)] * CLUSTERS
    ids = []
    for j in range(shares):
        note = in_ref[(j + 1) * width - 1:(j + 1) * width, :]
        ident = jnp.broadcast_to(note[:, 0:1], (1, LANES))
        count = jnp.broadcast_to(note[:, LANES - 1:LANES], (1, LANES))
        ids.append(ident)
        delta = in_ref[j * width:j * width + data, :]
        for c in range(CLUSTERS):
            weight = jnp.where(ident == c, count, 0.0)
            counts[c] = counts[c] + weight
            sums[c] = sums[c] + weight * delta
    sums = [total / (LR * count) for total, count in zip(sums, counts)]
    for j in range(shares):
        mine = sums[0]
        for c in range(1, CLUSTERS):
            mine = jnp.where(ids[j] == c, sums[c], mine)
        for k in range(tblocks):
            out_ref[j, :, k * LANES:(k + 1) * LANES] = mine[k * each:(k + 1) * each]


def on_device(features, targets, lower_weight, head_weight, batch_rows, sample_counts, cluster_ids):
    shares = lax.axis_size(AXES)
    pool_rows, inputs = features.shape[1:]
    hidden, outs = head_weight.shape[1:]
    chunk = 256
    each = hidden // shares
    tblocks = outs // LANES
    width = tblocks * each + 1
    smem = pl.BlockSpec(memory_space=pltpu.SMEM)
    hbm = pl.BlockSpec(memory_space=pltpu.HBM)
    vmem = pl.BlockSpec(memory_space=pltpu.VMEM)
    outgoing = pl.pallas_call(
        functools.partial(client_kernel, shares=shares, chunk=chunk),
        out_shape=jax.ShapeDtypeStruct((shares * width, LANES), F32),
        in_specs=[smem, smem, smem, hbm, hbm, hbm, hbm],
        out_specs=vmem,
        scratch_shapes=[
            pltpu.VMEM((pool_rows, inputs), BF16),
            pltpu.VMEM((inputs, hidden), BF16),
            pltpu.VMEM((pool_rows, outs), BF16),
            pltpu.VMEM((hidden, outs), F32),
            pltpu.VMEM((pool_rows * SUB, LANES), F32),
            pltpu.VMEM((2, chunk * SUB, LANES), F32),
            pltpu.VMEM((hidden, outs), F32),
            pltpu.VMEM((2, hidden, outs), BF16),
            pltpu.SemaphoreType.DMA((pool_rows // chunk + 3,)),
        ],
        compiler_params=pltpu.CompilerParams(vmem_limit_bytes=40 << 20),
        name="client",
    )(batch_rows[0], sample_counts, cluster_ids, features, lower_weight, targets, head_weight)
    arrived = lax.all_to_all(outgoing.reshape(shares * width, 1, LANES), AXES, split_axis=0, concat_axis=0, tiled=True)
    back = pl.pallas_call(
        functools.partial(cluster_kernel, shares=shares),
        out_shape=jax.ShapeDtypeStruct((shares, each, outs), F32),
        in_specs=[vmem],
        out_specs=vmem,
        name="cluster",
    )(arrived.reshape(shares * width, LANES))
    mine = lax.all_to_all(back, AXES, split_axis=0, concat_axis=0, tiled=True)
    return mine.reshape(head_weight.shape)


def solution(mesh):
    whole = P(AXES, None, None)
    return jax.shard_map(
        on_device,
        mesh=mesh,
        in_specs=(whole, whole, whole, whole, whole, P(AXES), P(AXES)),
        out_specs=whole,
        check_vma=False,
    )
```

time: 139 us -> 68.2 us (0.49)
  local copies, waits for them, and re-layouts: 29.7 us -> 7.16 us
  blocking collectives: 62.6 us -> 42 us
  matrix products: 20.5 us -> 0 us
  Pallas kernels: 0 us -> 17.3 us
  waiting for transfers between devices: 13 us -> 0 us
  starting transfers between devices: 10.4 us -> 0 us
    unnamed x1 -> x0, blocking collectives: 40 us -> none
    gather x4 -> x0, local copies, waits for them, and re-layouts: 23.9 us -> none  [the longest x2 15 us: on_device(): picked = jnp.take(hidden, batch_rows[0, step], axis=0)]
    dot_general x7 -> x0, matrix products: 20.5 us -> none  [the longest x2 7.26 us: on_device(): grad = jnp.dot(picked.T, err, precision=lax.Precision.HIGHEST) / count_rows]
    all_to_all x2, blocking collectives: 22.6 us -> 42 us  [the longest x1 23.5 us: on_device(): lax.all_to_all(outgoing.reshape(shares * width, 1, LANES), AXES, split_ax...]
    pallas_call x0 -> x2, Pallas kernels: none -> 17.3 us  [the longest x1 14.8 us: on_device(): pl.pallas_call(functools.partial(client_kernel, shares=shares, chunk=chun...]
    all_to_all x2 -> x0, waiting for transfers between devices: 13 us -> none  [the longest x1 13 us: on_device(): lax.all_to_all(lax.all_to_all(outgoing, 'chip', split_axis=0, concat_axis...]
    all_to_all x2 -> x0, starting transfers between devices: 10.4 us -> none  [the longest x1 5.94 us: on_device(): lax.all_to_all(lax.all_to_all(scaled, 'chip', split_axis=0, concat_axis=0...]
    unnamed x14 -> x11, local copies, waits for them, and re-layouts: 0.65 us -> 7.16 us
  transfers between devices with their start and end apart: 2 -> 0, of which waited for: 1 -> 0; matrix products, arithmetic and copies ran while one was open for 1% -> 0% of each run, Pallas kernels for 0% -> 0%
where the time goes in v1:
time: 68.2 us; the launch traced here: 67.8 us
  blocking collectives  42 us (62%)
  Pallas kernels  17.3 us (25%)
  local copies, waits for them, and re-layouts  7.16 us (10%)
  between operations  1.32 us (2%)
    all_to_all x1, blocking collectives, on_device(): lax.all_to_all(outgoing.reshape(shares * width, 1, LANES), AXES, split_ax...  23.5 us
    all_to_all x1, blocking collectives, on_device(): mine = lax.all_to_all(back, AXES, split_axis=0, concat_axis=0, tiled=True)  18.5 us
    pallas_call x1, Pallas kernels, on_device(): pl.pallas_call(functools.partial(client_kernel, shares=shares, chunk=chun...  14.8 us
    unnamed x11, local copies, waits for them, and re-layouts  7.16 us
    pallas_call x1, Pallas kernels, on_device(): pl.pallas_call(functools.partial(cluster_kernel, shares=shares), out_shap...  2.54 us

profile of v1, /device:TPU:0, one launch (start us, length us, event | category | flops | bytes accessed | tf_op | source)
XLA Modules:
  0.0 67.8 jit_solution(10416242310803257218)
XLA Ops:
  1.3 0.0 copy-start
  1.3 2.2 %copy-done = bf16[1,2048,1024]{2,1,0:T(8,128)(2,1)S(1)} copy-done((bf16[1,2048,1024]{2,1,0:T(8,128)(2,1)S(1)}, bf16[1,2048,1024]{2,1,0:T(8,128)(2,1)}, u32[]{:S(2)}) %copy-start) | copy-done | bytes 4194328
  3.5 0.0 copy-start.1
  3.5 1.2 %copy-done.1 = bf16[1,1024,512]{2,1,0:T(8,128)(2,1)S(1)} copy-done((bf16[1,1024,512]{2,1,0:T(8,128)(2,1)S(1)}, bf16[1,1024,512]{2,1,0:T(8,128)(2,1)}, u32[]{:S(2)}) %copy-start.1) | copy-done | bytes 1048600
  4.7 0.0 copy-start.2
  4.7 1.2 %copy-done.2 = bf16[1,2048,256]{2,1,0:T(8,128)(2,1)S(1)} copy-done((bf16[1,2048,256]{2,1,0:T(8,128)(2,1)S(1)}, bf16[1,2048,256]{2,1,0:T(8,128)(2,1)}, u32[]{:S(2)}) %copy-start.2) | copy-done | bytes 1048600
  5.9 0.0 copy-start.3
  5.9 1.0 %copy-done.3 = f32[1,512,256]{2,1,0:T(8,128)S(1)} copy-done((f32[1,512,256]{2,1,0:T(8,128)S(1)}, f32[1,512,256]{2,1,0:T(8,128)}, u32[]{:S(2)}) %copy-start.3) | copy-done | bytes 524312
  7.0 0.0 copy-start.4
  7.0 0.7 %copy-done.4 = s32[1,2,1024]{2,1,0:T(2,128)S(1)} copy-done((s32[1,2,1024]{2,1,0:T(2,128)S(1)}, s32[1,2,1024]{2,1,0:T(2,128)}, u32[]{:S(2)}) %copy-start.4) | copy-done | bytes 8216
  7.7 14.8 %client.1 = f32[1056,128]{1,0:T(8,128)S(1)} custom-call(s32[2,1024]{1,0:T(2,128)S(1)} %bitcast.7, s32[1]{0:T(128)S(6)} %copy.10.count_ref, s32[1]{0:T(128)S(6)} %copy.11.cluster_ref, bf16[1,2048,1024]{2,1,0:T(8,128)(2,1)S(1)} %copy-done, bf16[1,1024,512]{2,1,0:T(8,128)(2,1)S(1)} %copy-done.1, bf16[1,2048,256]{2,1,0:T(8,128)(2,1)S(1)} %copy-done.2, ...), custom_call_target="tpu_custom_call" | custom-call | tf_op jit(solution)/shard_map/client/pallas_call | solution.py:156
  22.5 23.5 %all_to_all.10 = f32[1056,1,128]{2,1,0:T(1,128)} all-to-all(f32[1056,1,128]{2,1,0:T(1,128)S(1)} %bitcast.6), channel_id=1, replica_groups=mesh['chip'=2,'board'=4,'cuts'=4] {'chip','board','cuts'}, dimensions={0} | all-to-all | bytes 1081344 | tf_op jit(solution)/shard_map/all_to_all | solution.py:175
  45.9 2.5 %cluster.1 = f32[32,16,256]{2,1,0:T(8,128)} custom-call(f32[1056,128]{1,0:T(8,128)} %bitcast.8), custom_call_target="tpu_custom_call" | custom-call | tf_op jit(solution)/shard_map/cluster/pallas_call | solution.py:176
  48.5 18.5 %all_to_all.11 = f32[32,16,256]{2,1,0:T(8,128)S(1)} all-to-all(f32[32,16,256]{2,1,0:T(8,128)} %cluster.1), channel_id=1, replica_groups=mesh['chip'=2,'board'=4,'cuts'=4] {'chip','board','cuts'}, dimensions={0} | all-to-all | bytes 1048576 | tf_op jit(solution)/shard_map/all_to_all | solution.py:183
  67.0 0.8 %copy.12 = f32[1,512,256]{2,1,0:T(8,128)} copy(f32[1,512,256]{2,1,0:T(8,128)S(1)} %bitcast.9) | data formatting | bytes 1048576
Async XLA Ops:
  1.3 2.2 %copy-start = (bf16[1,2048,1024]{2,1,0:T(8,128)(2,1)S(1)}, bf16[1,2048,1024]{2,1,0:T(8,128)(2,1)}, u32[]{:S(2)}) copy-start(bf16[1,2048,1024]{2,1,0:T(8,128)(2,1)} %features_ref.1) | copy-start | bytes 12582916
  3.5 1.2 %copy-start.1 = (bf16[1,1024,512]{2,1,0:T(8,128)(2,1)S(1)}, bf16[1,1024,512]{2,1,0:T(8,128)(2,1)}, u32[]{:S(2)}) copy-start(bf16[1,1024,512]{2,1,0:T(8,128)(2,1)} %lower_ref.1) | copy-start | bytes 3145732
  4.7 1.2 %copy-start.2 = (bf16[1,2048,256]{2,1,0:T(8,128)(2,1)S(1)}, bf16[1,2048,256]{2,1,0:T(8,128)(2,1)}, u32[]{:S(2)}) copy-start(bf16[1,2048,256]{2,1,0:T(8,128)(2,1)} %targets_ref.1) | copy-start | bytes 3145732
  5.9 1.0 %copy-start.3 = (f32[1,512,256]{2,1,0:T(8,128)S(1)}, f32[1,512,256]{2,1,0:T(8,128)}, u32[]{:S(2)}) copy-start(f32[1,512,256]{2,1,0:T(8,128)} %head_ref.1) | copy-start | bytes 1572868
  7.0 0.7 %copy-start.4 = (s32[1,2,1024]{2,1,0:T(2,128)S(1)}, s32[1,2,1024]{2,1,0:T(2,128)}, u32[]{:S(2)}) copy-start(s32[1,2,1024]{2,1,0:T(2,128)} %param.11) | copy-start | bytes 24580

commit v2 on v1

v2 whole, which is shorter than its diff:
```python
import functools

import jax
import jax.numpy as jnp
from jax import lax
from jax.experimental import pallas as pl
from jax.experimental.pallas import tpu as pltpu
from jax.sharding import PartitionSpec as P

LR = 0.5
CLUSTERS = 8
LANES = 128
SUB = 8
PITCH = 9
VMEM_LIMIT = 65_500_000
AXES = ("chip", "board", "cuts")
F32 = jnp.float32
BF16 = jnp.bfloat16


def halves(value):
    high = value.astype(BF16)
    return high, (value - high.astype(F32)).astype(BF16)


def client_kernel(
    rows_hbm, count_ref, cluster_ref, features_ref, lower_ref, targets_ref, head_ref, out_ref,
    rows_ref, feat, low, targ, start, pool, picked_a, picked_b,
    first, total, begin, weight, arrived, *, shares, chunk,
):
    pool_rows, hidden = feat.shape[0], low.shape[1]
    steps, count_rows = rows_hbm.shape[1:]
    outs = targ.shape[1]
    blocks, tblocks = hidden // LANES, outs // LANES
    chunks = pool_rows // chunk
    scale = -(LR / count_rows)

    def part(i):
        at = pl.ds(i * chunk, chunk)
        return pltpu.make_async_copy(features_ref.at[0, at], feat.at[at], arrived.at[i])

    def whole(source, target, i):
        return pltpu.make_async_copy(source, target, arrived.at[chunks + i])

    low_copy = whole(lower_ref.at[0], low, 0)
    targ_copy = whole(targets_ref.at[0], targ, 1)
    late = [
        whole(head_ref.at[0], start, 2),
        *[whole(rows_hbm.at[0, s], rows_ref.at[pl.ds(s * count_rows, count_rows)], 3 + s) for s in range(steps)],
    ]
    ahead = 2
    low_copy.start()
    for i in range(ahead):
        part(i).start()
    low_copy.wait()
    for i in range(ahead, 2 * ahead):
        part(i).start()

    def sample(i, with_targets):
        part(i).wait()
        at = pl.ds(pl.multiple_of(i * chunk, chunk), chunk)
        h = jnp.tanh(jnp.dot(feat[at, :], low[...], preferred_element_type=F32))
        for k in range(blocks):
            pool[pl.ds(i * chunk * PITCH + k, chunk, stride=PITCH), :] = h[:, k * LANES:(k + 1) * LANES]
        for j in range(2 if with_targets else 0):
            c = 2 * i - chunks + j
            t = targ[pl.ds(pl.multiple_of(c * chunk, chunk), chunk), :].astype(F32)
            for k in range(tblocks):
                pool[pl.ds(c * chunk * PITCH + blocks + k, chunk, stride=PITCH), :] = t[:, k * LANES:(k + 1) * LANES]

    @pl.loop(0, chunks // 2)
    def _(i):
        part(i + 2 * ahead).start()

        @pl.when(i == 1)
        def _():
            targ_copy.start()
            for copy in late:
                copy.start()

        sample(i, False)

    targ_copy.wait()

    @pl.loop(chunks // 2, chunks)
    def _(i):
        @pl.when(i + 2 * ahead < chunks)
        def _():
            part(i + 2 * ahead).start()

        sample(i, True)

    for copy in late:
        copy.wait()

    per_step = count_rows // chunk

    def pick(i, into):
        for r in range(chunk):
            row = rows_ref[i * chunk + r]
            into[r * PITCH:r * PITCH + SUB, :] = pool[pl.ds(row * PITCH, SUB), :]

    def picks(source):
        h = jnp.concatenate([source[pl.ds(k, chunk, stride=PITCH), :] for k in range(blocks)], axis=1)
        t = jnp.concatenate([source[pl.ds(blocks + k, chunk, stride=PITCH), :] for k in range(tblocks)], axis=1)
        return (*halves(h), t.astype(BF16))

    def load_weight(value):
        w_high, w_rest = halves(value)
        weight[:, :hidden] = w_high
        weight[:, hidden:2 * hidden] = w_rest
        weight[:, 2 * hidden:3 * hidden] = w_high

    def errors(h, rest, t):
        e = lax.dot_general(
            weight[...], jnp.concatenate([h, h, rest, t], axis=1), (((1,), (1,)), ((), ())), preferred_element_type=F32
        )
        return halves(e)

    start_t = start[...].T
    begin[...] = start_t
    load_weight(start_t)
    row_at = lax.broadcasted_iota(jnp.int32, (outs, outs), 0)
    lane_at = lax.broadcasted_iota(jnp.int32, (outs, outs), 1)
    weight[:, 3 * hidden:] = jnp.where(row_at == lane_at, -1.0, 0.0).astype(BF16)
    total[...] = jnp.zeros_like(total)
    pick(0, picked_a)
    last = steps * per_step - 1

    for step in range(steps):
        @pl.loop(0, per_step // 2)
        def _(j):
            i = step * per_step + 2 * j
            pick(i + 1, picked_b)
            h_a, rest_a, t_a = picks(picked_a)
            e_a, d_a = errors(h_a, rest_a, t_a)
            h_b, rest_b, t_b = picks(picked_b)
            e_b, d_b = errors(h_b, rest_b, t_b)
            total[...] += jnp.dot(
                jnp.concatenate([e_a, d_a, e_a, e_b, d_b, e_b], axis=1),
                jnp.concatenate([h_a, h_a, rest_a, h_b, h_b, rest_b], axis=0),
                preferred_element_type=F32,
            )
            pick(jnp.minimum(i + 2, last), picked_a)

        if step + 1 < steps:
            load_weight(begin[...] + scale * total[...])
    first[...] = total[...].T

    each = hidden // shares
    width = tblocks * each + 1
    lane = lax.broadcasted_iota(jnp.int32, (1, LANES), 1)
    note = jnp.where(lane < LANES // 2, cluster_ref[0], count_ref[0]).astype(F32)
    for s in range(shares):
        for k in range(tblocks):
            out_ref[s * width + k * each:s * width + (k + 1) * each, :] = (
                first[s * each:(s + 1) * each, k * LANES:(k + 1) * LANES] * scale
            )
        out_ref[(s + 1) * width - 1:(s + 1) * width, :] = note


def cluster_kernel(in_ref, out_ref, *, shares):
    each, outs = out_ref.shape[1], out_ref.shape[2]
    tblocks = outs // LANES
    data = tblocks * each
    width = data + 1
    full = (data, LANES)
    sums = [jnp.zeros(full, F32)] * CLUSTERS
    counts = [jnp.zeros((1, LANES), F32)] * CLUSTERS
    ids = []
    for j in range(shares):
        note = in_ref[(j + 1) * width - 1:(j + 1) * width, :]
        ident = jnp.broadcast_to(note[:, 0:1], (1, LANES))
        count = jnp.broadcast_to(note[:, LANES - 1:LANES], (1, LANES))
        ids.append(ident)
        delta = in_ref[j * width:j * width + data, :]
        for c in range(CLUSTERS):
            weight = jnp.where(ident == c, count, 0.0)
            counts[c] = counts[c] + weight
            sums[c] = sums[c] + weight * delta
    sums = [total / (LR * count) for total, count in zip(sums, counts)]
    for j in range(shares):
        mine = sums[0]
        for c in range(1, CLUSTERS):
            mine = jnp.where(ids[j] == c, sums[c], mine)
        for k in range(tblocks):
            out_ref[j, :, k * LANES:(k + 1) * LANES] = mine[k * each:(k + 1) * each]


def on_device(features, targets, lower_weight, head_weight, batch_rows, sample_counts, cluster_ids):
    shares = lax.axis_size(AXES)
    pool_rows, inputs = features.shape[1:]
    hidden, outs = head_weight.shape[1:]
    chunk = 256
    each = hidden // shares
    tblocks = outs // LANES
    width = tblocks * each + 1
    smem = pl.BlockSpec(memory_space=pltpu.SMEM)
    hbm = pl.BlockSpec(memory_space=pltpu.HBM)
    vmem = pl.BlockSpec(memory_space=pltpu.VMEM)
    steps, count_rows = batch_rows.shape[1:]
    outgoing = pl.pallas_call(
        functools.partial(client_kernel, shares=shares, chunk=chunk),
        out_shape=jax.ShapeDtypeStruct((shares * width, LANES), F32),
        in_specs=[hbm, smem, smem, hbm, hbm, hbm, hbm],
        out_specs=vmem,
        scratch_shapes=[
            pltpu.SMEM((steps * count_rows,), jnp.int32),
            pltpu.VMEM((pool_rows, inputs), BF16),
            pltpu.VMEM((inputs, hidden), BF16),
            pltpu.VMEM((pool_rows, outs), BF16),
            pltpu.VMEM((hidden, outs), F32),
            pltpu.VMEM((pool_rows * PITCH, LANES), F32),
            pltpu.VMEM((chunk * PITCH, LANES), F32),
            pltpu.VMEM((chunk * PITCH, LANES), F32),
            pltpu.VMEM((hidden, outs), F32),
            pltpu.VMEM((outs, hidden), F32),
            pltpu.VMEM((outs, hidden), F32),
            pltpu.VMEM((outs, 3 * hidden + outs), BF16),
            pltpu.SemaphoreType.DMA((pool_rows // chunk + 3 + steps,)),
        ],
        compiler_params=pltpu.CompilerParams(vmem_limit_bytes=VMEM_LIMIT),
        name="client",
    )(batch_rows, sample_counts, cluster_ids, features, lower_weight, targets, head_weight)
    arrived = lax.all_to_all(outgoing.reshape(shares * width, 1, LANES), AXES, split_axis=0, concat_axis=0, tiled=True)
    back = pl.pallas_call(
        functools.partial(cluster_kernel, shares=shares),
        out_shape=jax.ShapeDtypeStruct((shares, each, outs), F32),
        in_specs=[vmem],
        out_specs=vmem,
        compiler_params=pltpu.CompilerParams(vmem_limit_bytes=8 << 20),
        name="cluster",
    )(arrived.reshape(shares * width, LANES))
    mine = lax.all_to_all(back, AXES, split_axis=0, concat_axis=0, tiled=True)
    return mine.reshape(head_weight.shape)


def solution(mesh):
    whole = P(AXES, None, None)
    return jax.shard_map(
        on_device,
        mesh=mesh,
        in_specs=(whole, whole, whole, whole, whole, P(AXES), P(AXES)),
        out_specs=whole,
        check_vma=False,
    )
```

time: 68.2 us -> 56.9 us (0.83)
  local copies, waits for them, and re-layouts: 7.16 us -> 0.79 us
  Pallas kernels: 17.3 us -> 13 us
    unnamed x11 -> x1, local copies, waits for them, and re-layouts: 7.16 us -> 0.79 us
    pallas_call x1, Pallas kernels: 14.8 us -> 12.3 us  [on_device(): pl.pallas_call(functools.partial(client_kernel, shares=shares, chunk=chun...]
    pallas_call x1, Pallas kernels: 2.54 us -> 0.68 us  [on_device(): pl.pallas_call(functools.partial(cluster_kernel, shares=shares), out_shap...]
where the time goes in v2:
time: 56.9 us; the launch traced here: 56.6 us
  blocking collectives  41.6 us (73%)
  Pallas kernels  13 us (23%)
  between operations  1.31 us (2%)
  local copies, waits for them, and re-layouts  0.79 us (1%)
    all_to_all x1, blocking collectives, on_device(): lax.all_to_all(outgoing.reshape(shares * width, 1, LANES), AXES, split_ax...  23.6 us
    all_to_all x1, blocking collectives, on_device(): mine = lax.all_to_all(back, AXES, split_axis=0, concat_axis=0, tiled=True)  18 us
    pallas_call x1, Pallas kernels, on_device(): pl.pallas_call(functools.partial(client_kernel, shares=shares, chunk=chun...  12.3 us

profile of v2, /device:TPU:0, one launch (start us, length us, event | category | flops | bytes accessed | tf_op | source)
XLA Modules:
  0.0 56.6 jit_solution(12318205452305838033)
XLA Ops:
  1.3 12.3 %client.1 = f32[1056,128]{1,0:T(8,128)} custom-call(s32[1,2,1024]{2,1,0:T(2,128)} %rows_hbm.1, s32[1]{0:T(128)S(6)} %copy.10.count_ref, s32[1]{0:T(128)S(6)} %copy.11.cluster_ref, bf16[1,2048,1024]{2,1,0:T(8,128)(2,1)} %features_ref.1, bf16[1,1024,512]{2,1,0:T(8,128)(2,1)} %lower_ref.1, bf16[1,2048,256]{2,1,0:T(8,128)(2,1)} %targets_ref.1, ...), custom_call_target="tpu_custom_call" | custom-call | tf_op jit(solution)/shard_map/client/pallas_call | solution.py:202
  13.6 23.6 %all_to_all.10 = f32[1056,1,128]{2,1,0:T(1,128)S(1)} all-to-all(f32[1056,1,128]{2,1,0:T(1,128)} %bitcast.6), channel_id=1, replica_groups=mesh['chip'=2,'board'=4,'cuts'=4] {'chip','board','cuts'}, dimensions={0} | all-to-all | bytes 1081344 | tf_op jit(solution)/shard_map/all_to_all | solution.py:225
  37.2 0.7 %cluster.1 = f32[32,16,256]{2,1,0:T(8,128)S(1)} custom-call(f32[1056,128]{1,0:T(8,128)S(1)} %bitcast.5), custom_call_target="tpu_custom_call" | custom-call | tf_op jit(solution)/shard_map/cluster/pallas_call | solution.py:226
  37.9 18.0 %all_to_all.11 = f32[32,16,256]{2,1,0:T(8,128)S(1)} all-to-all(f32[32,16,256]{2,1,0:T(8,128)S(1)} %cluster.1), channel_id=1, replica_groups=mesh['chip'=2,'board'=4,'cuts'=4] {'chip','board','cuts'}, dimensions={0} | all-to-all | bytes 1048576 | tf_op jit(solution)/shard_map/all_to_all | solution.py:234
  55.9 0.8 %copy.12 = f32[1,512,256]{2,1,0:T(8,128)} copy(f32[1,512,256]{2,1,0:T(8,128)S(1)} %bitcast.7) | data formatting | bytes 1048576

commit v3 on v2

v3 whole, which is shorter than its diff:
```python
import functools

import jax
import jax.numpy as jnp
from jax import lax
from jax.experimental import pallas as pl
from jax.experimental.pallas import tpu as pltpu
from jax.sharding import PartitionSpec as P

LR = 0.5
CLUSTERS = 8
LANES = 128
SUB = 8
PITCH = 9
VMEM_LIMIT = 40 << 20
AXES = ("chip", "board", "cuts")
F32 = jnp.float32
BF16 = jnp.bfloat16


def halves(value):
    high = value.astype(BF16)
    return high, (value - high.astype(F32)).astype(BF16)


def client_kernel(
    rows_hbm, count_ref, cluster_ref, features_ref, lower_ref, targets_ref, head_ref, out_ref,
    rows_ref, places, feat, low, targ, start, pool, picked_a, picked_b,
    first, total, begin, weight, minus, arrived, *, shares, chunk,
):
    pool_rows, hidden = feat.shape[0], low.shape[1]
    steps, count_rows = rows_hbm.shape[1:]
    outs = targ.shape[1]
    blocks, tblocks = hidden // LANES, outs // LANES
    scale = -(LR / count_rows)
    sizes = [chunk] * 2 + [2 * chunk] * ((pool_rows - 2 * chunk) // (2 * chunk))
    sizes += [pool_rows - sum(sizes)] * (sum(sizes) < pool_rows)
    offsets = [sum(sizes[:i]) for i in range(len(sizes))]

    def whole(source, target, i):
        return pltpu.make_async_copy(source, target, arrived.at[i])

    parts = [
        whole(features_ref.at[0, pl.ds(o, n)], feat.at[pl.ds(o, n)], i) for i, (o, n) in enumerate(zip(offsets, sizes))
    ]
    free = len(parts)
    low_copy = whole(lower_ref.at[0], low, free)
    targ_copy = whole(targets_ref.at[0], targ, free + 1)
    head_copy = whole(head_ref.at[0], start, free + 2)
    rows_copy = whole(rows_hbm.at[0], places, free + 3)
    moved = [whole(places.at[s], rows_ref.at[pl.ds(s * count_rows, count_rows)], free + 4 + s) for s in range(steps)]
    low_copy.start()
    for copy in parts[:2]:
        copy.start()
    low_copy.wait()
    parts[2].start()
    rows_copy.start()
    for i, (o, n) in enumerate(zip(offsets, sizes)):
        parts[i].wait()
        if i + 3 < len(parts):
            parts[i + 3].start()
        if i + 4 == len(parts):
            targ_copy.start()
            head_copy.start()
        if i == 2:
            rows_copy.wait()
            places[...] = places[...] * PITCH
        if i == 3:
            for copy in moved:
                copy.start()
        h = jnp.tanh(jnp.dot(feat[o:o + n, :], low[...], preferred_element_type=F32))
        for k in range(blocks):
            pool[pl.ds(o * PITCH + k, n, stride=PITCH), :] = h[:, k * LANES:(k + 1) * LANES]
    targ_copy.wait()
    head_copy.wait()
    for copy in moved:
        copy.wait()
    for k in range(tblocks):
        t = targ[:, k * LANES:(k + 1) * LANES].astype(F32)
        pool[pl.ds(blocks + k, pool_rows, stride=PITCH), :] = t

    per_step = count_rows // chunk

    def pick(i, into):
        for r in range(chunk):
            at = rows_ref[i * chunk + r]
            into[r * PITCH:r * PITCH + SUB, :] = pool[pl.ds(at, SUB), :]

    def picks(source):
        h = jnp.concatenate([source[pl.ds(k, chunk, stride=PITCH), :] for k in range(blocks)], axis=1)
        t = jnp.concatenate([source[pl.ds(blocks + k, chunk, stride=PITCH), :] for k in range(tblocks)], axis=1)
        return (*halves(h), t.astype(BF16))

    def load_weight(value):
        w_high, w_rest = halves(value)
        weight[:outs] = w_high
        weight[outs:] = w_rest

    def errors(h, rest, t):
        dot = functools.partial(lax.dot_general, dimension_numbers=(((1,), (1,)), ((), ())), preferred_element_type=F32)
        both = dot(weight[...], h)
        e = both[:outs] + (both[outs:] + dot(weight[:outs], rest)) + dot(minus[...], t)
        return halves(e)

    start_t = start[...].T
    begin[...] = start_t
    load_weight(start_t)
    row_at = lax.broadcasted_iota(jnp.int32, (outs, outs), 0)
    lane_at = lax.broadcasted_iota(jnp.int32, (outs, outs), 1)
    minus[...] = jnp.where(row_at == lane_at, -1.0, 0.0).astype(BF16)
    pick(0, picked_a)
    pick(1, picked_b)

    for step in range(steps):
        @pl.when(rows_ref[0] >= 0)
        def _():
            for i in range(step * per_step, (step + 1) * per_step, 2):
                h_a, rest_a, t_a = picks(picked_a)
                e_a, d_a = errors(h_a, rest_a, t_a)
                h_b, rest_b, t_b = picks(picked_b)
                e_b, d_b = errors(h_b, rest_b, t_b)
                if i + 2 < steps * per_step:
                    pick(i + 2, picked_a)
                    pick(i + 3, picked_b)
                grad = jnp.dot(
                    jnp.concatenate([e_a, d_a, e_a, e_b, d_b, e_b], axis=1),
                    jnp.concatenate([h_a, h_a, rest_a, h_b, h_b, rest_b], axis=0),
                    preferred_element_type=F32,
                )
                total[...] = grad if i == 0 else total[...] + grad
            if step + 1 < steps:
                load_weight(begin[...] + scale * total[...])

    first[...] = total[...].T

    each = hidden // shares
    width = tblocks * each + 1
    lane = lax.broadcasted_iota(jnp.int32, (1, LANES), 1)
    note = jnp.where(lane < LANES // 2, cluster_ref[0], count_ref[0]).astype(F32)
    for s in range(shares):
        for k in range(tblocks):
            out_ref[s * width + k * each:s * width + (k + 1) * each, :] = (
                first[s * each:(s + 1) * each, k * LANES:(k + 1) * LANES] * scale
            )
        out_ref[(s + 1) * width - 1:(s + 1) * width, :] = note


def cluster_kernel(in_ref, out_ref, *, shares):
    each, outs = out_ref.shape[1], out_ref.shape[2]
    tblocks = outs // LANES
    data = tblocks * each
    width = data + 1
    full = (data, LANES)
    sums = [jnp.zeros(full, F32)] * CLUSTERS
    counts = [jnp.zeros((1, LANES), F32)] * CLUSTERS
    ids = []
    for j in range(shares):
        note = in_ref[(j + 1) * width - 1:(j + 1) * width, :]
        ident = jnp.broadcast_to(note[:, 0:1], (1, LANES))
        count = jnp.broadcast_to(note[:, LANES - 1:LANES], (1, LANES))
        ids.append(ident)
        delta = in_ref[j * width:j * width + data, :]
        for c in range(CLUSTERS):
            weight = jnp.where(ident == c, count, 0.0)
            counts[c] = counts[c] + weight
            sums[c] = sums[c] + weight * delta
    sums = [total / (LR * count) for total, count in zip(sums, counts)]
    for j in range(shares):
        mine = sums[0]
        for c in range(1, CLUSTERS):
            mine = jnp.where(ids[j] == c, sums[c], mine)
        for k in range(tblocks):
            out_ref[j, :, k * LANES:(k + 1) * LANES] = mine[k * each:(k + 1) * each]


def on_device(features, targets, lower_weight, head_weight, batch_rows, sample_counts, cluster_ids):
    shares = lax.axis_size(AXES)
    pool_rows, inputs = features.shape[1:]
    hidden, outs = head_weight.shape[1:]
    chunk = 256
    each = hidden // shares
    tblocks = outs // LANES
    width = tblocks * each + 1
    smem = pl.BlockSpec(memory_space=pltpu.SMEM)
    hbm = pl.BlockSpec(memory_space=pltpu.HBM)
    vmem = pl.BlockSpec(memory_space=pltpu.VMEM)
    steps, count_rows = batch_rows.shape[1:]
    far = functools.partial(pltpu.with_memory_space_constraint, memory_space=pltpu.HBM)
    outgoing = pl.pallas_call(
        functools.partial(client_kernel, shares=shares, chunk=chunk),
        out_shape=jax.ShapeDtypeStruct((shares * width, LANES), F32),
        in_specs=[hbm, smem, smem, hbm, hbm, hbm, hbm],
        out_specs=vmem,
        scratch_shapes=[
            pltpu.SMEM((steps * count_rows,), jnp.int32),
            pltpu.VMEM((steps, count_rows), jnp.int32),
            pltpu.VMEM((pool_rows, inputs), BF16),
            pltpu.VMEM((inputs, hidden), BF16),
            pltpu.VMEM((pool_rows, outs), BF16),
            pltpu.VMEM((hidden, outs), F32),
            pltpu.VMEM((pool_rows * PITCH, LANES), F32),
            pltpu.VMEM((chunk * PITCH, LANES), F32),
            pltpu.VMEM((chunk * PITCH, LANES), F32),
            pltpu.VMEM((hidden, outs), F32),
            pltpu.VMEM((outs, hidden), F32),
            pltpu.VMEM((outs, hidden), F32),
            pltpu.VMEM((2 * outs, hidden), BF16),
            pltpu.VMEM((outs, outs), BF16),
            pltpu.SemaphoreType.DMA((pool_rows // chunk + 4 + steps,)),
        ],
        compiler_params=pltpu.CompilerParams(vmem_limit_bytes=VMEM_LIMIT),
        name="client",
    )(
        far(batch_rows), sample_counts, cluster_ids, far(features), far(lower_weight), far(targets), far(head_weight)
    )
    arrived = lax.all_to_all(outgoing.reshape(shares * width, 1, LANES), AXES, split_axis=0, concat_axis=0, tiled=True)
    back = pl.pallas_call(
        functools.partial(cluster_kernel, shares=shares),
        out_shape=jax.ShapeDtypeStruct((shares, each, outs), F32),
        in_specs=[vmem],
        out_specs=vmem,
        compiler_params=pltpu.CompilerParams(vmem_limit_bytes=8 << 20),
        name="cluster",
    )(arrived.reshape(shares * width, LANES))
    mine = lax.all_to_all(back, AXES, split_axis=0, concat_axis=0, tiled=True)
    return mine.reshape(head_weight.shape)


def solution(mesh):
    whole = P(AXES, None, None)
    return jax.shard_map(
        on_device,
        mesh=mesh,
        in_specs=(whole, whole, whole, whole, whole, P(AXES), P(AXES)),
        out_specs=whole,
        check_vma=False,
    )
```

time: 56.9 us -> 54.9 us (0.965)
  Pallas kernels: 13 us -> 11.2 us
    pallas_call x1, Pallas kernels: 12.3 us -> 10.5 us  [on_device(): pl.pallas_call(functools.partial(client_kernel, shares=shares, chunk=chun...]
where the time goes in v3:
time: 54.9 us; the launch traced here: 54.7 us
  blocking collectives  41.4 us (75%)
  Pallas kernels  11.2 us (20%)
  between operations  1.31 us (2%)
  local copies, waits for them, and re-layouts  0.79 us (1%)
    all_to_all x1, blocking collectives, on_device(): lax.all_to_all(outgoing.reshape(shares * width, 1, LANES), AXES, split_ax...  23.4 us
    all_to_all x1, blocking collectives, on_device(): mine = lax.all_to_all(back, AXES, split_axis=0, concat_axis=0, tiled=True)  18 us
    pallas_call x1, Pallas kernels, on_device(): pl.pallas_call(functools.partial(client_kernel, shares=shares, chunk=chun...  10.5 us

profile of v3, /device:TPU:0, one launch (start us, length us, event | category | flops | bytes accessed | tf_op | source)
XLA Modules:
  0.0 54.7 jit_solution(12493680456750855666)
XLA Ops:
  1.3 10.5 %client.1 = f32[1056,128]{1,0:T(8,128)S(1)} custom-call(s32[1,2,1024]{2,1,0:T(2,128)} %rows_hbm.1, s32[1]{0:T(128)S(6)} %copy.10.count_ref, s32[1]{0:T(128)S(6)} %copy.11.cluster_ref, bf16[1,2048,1024]{2,1,0:T(8,128)(2,1)} %features_ref.1, bf16[1,1024,512]{2,1,0:T(8,128)(2,1)} %lower_ref.1, bf16[1,2048,256]{2,1,0:T(8,128)(2,1)} %targets_ref.1, ...), custom_call_target="tpu_custom_call" | custom-call | tf_op jit(solution)/shard_map/client/pallas_call | solution.py:189
  11.8 23.4 %all_to_all.10 = f32[1056,1,128]{2,1,0:T(1,128)S(1)} all-to-all(f32[1056,1,128]{2,1,0:T(1,128)S(1)} %bitcast.5), channel_id=1, replica_groups=mesh['chip'=2,'board'=4,'cuts'=4] {'chip','board','cuts'}, dimensions={0} | all-to-all | bytes 1081344 | tf_op jit(solution)/shard_map/all_to_all | solution.py:216
  35.2 0.7 %cluster.1 = f32[32,16,256]{2,1,0:T(8,128)S(1)} custom-call(f32[1056,128]{1,0:T(8,128)S(1)} %bitcast.6), custom_call_target="tpu_custom_call" | custom-call | tf_op jit(solution)/shard_map/cluster/pallas_call | solution.py:217
  35.9 18.0 %all_to_all.11 = f32[32,16,256]{2,1,0:T(8,128)S(1)} all-to-all(f32[32,16,256]{2,1,0:T(8,128)S(1)} %cluster.1), channel_id=1, replica_groups=mesh['chip'=2,'board'=4,'cuts'=4] {'chip','board','cuts'}, dimensions={0} | all-to-all | bytes 1048576 | tf_op jit(solution)/shard_map/all_to_all | solution.py:225
  53.9 0.8 %copy.12 = f32[1,512,256]{2,1,0:T(8,128)} copy(f32[1,512,256]{2,1,0:T(8,128)S(1)} %bitcast.7) | data formatting | bytes 1048576

commit v4 on v3

--- a/solution.py
+++ b/solution.py
@@ -26,7 +26,7 @@
 def client_kernel(
     rows_hbm, count_ref, cluster_ref, features_ref, lower_ref, targets_ref, head_ref, out_ref,
     rows_ref, places, feat, low, targ, start, pool, picked_a, picked_b,
-    first, total, begin, weight, minus, arrived, *, shares, chunk,
+    first, total, begin, weight, arrived, *, shares, chunk,
 ):
     pool_rows, hidden = feat.shape[0], low.shape[1]
     steps, count_rows = rows_hbm.shape[1:]
@@ -89,7 +89,7 @@
     def picks(source):
         h = jnp.concatenate([source[pl.ds(k, chunk, stride=PITCH), :] for k in range(blocks)], axis=1)
         t = jnp.concatenate([source[pl.ds(blocks + k, chunk, stride=PITCH), :] for k in range(tblocks)], axis=1)
-        return (*halves(h), t.astype(BF16))
+        return (*halves(h), t)
 
     def load_weight(value):
         w_high, w_rest = halves(value)
@@ -98,16 +98,13 @@
 
     def errors(h, rest, t):
         dot = functools.partial(lax.dot_general, dimension_numbers=(((1,), (1,)), ((), ())), preferred_element_type=F32)
-        both = dot(weight[...], h)
-        e = both[:outs] + (both[outs:] + dot(weight[:outs], rest)) + dot(minus[...], t)
+        w = weight[...]
+        e = dot(jnp.concatenate([w[:outs], w[outs:], w[:outs]], axis=1), jnp.concatenate([h, h, rest], axis=1)) - t.T
         return halves(e)
 
     start_t = start[...].T
     begin[...] = start_t
     load_weight(start_t)
-    row_at = lax.broadcasted_iota(jnp.int32, (outs, outs), 0)
-    lane_at = lax.broadcasted_iota(jnp.int32, (outs, outs), 1)
-    minus[...] = jnp.where(row_at == lane_at, -1.0, 0.0).astype(BF16)
     pick(0, picked_a)
     pick(1, picked_b)
 
@@ -205,7 +202,6 @@
             pltpu.VMEM((outs, hidden), F32),
             pltpu.VMEM((outs, hidden), F32),
             pltpu.VMEM((2 * outs, hidden), BF16),
-            pltpu.VMEM((outs, outs), BF16),
             pltpu.SemaphoreType.DMA((pool_rows // chunk + 4 + steps,)),
         ],
         compiler_params=pltpu.CompilerParams(vmem_limit_bytes=VMEM_LIMIT),

time: 54.9 us -> 54.5 us (level)
  no operation moved by 1% of the time
where the time goes in v4:
time: 54.5 us; the launch traced here: 54.3 us
  blocking collectives  41.4 us (76%)
  Pallas kernels  10.8 us (20%)
  between operations  1.31 us (2%)
  local copies, waits for them, and re-layouts  0.79 us (1%)
    all_to_all x1, blocking collectives, on_device(): lax.all_to_all(outgoing.reshape(shares * width, 1, LANES), AXES, split_ax...  23.4 us
    all_to_all x1, blocking collectives, on_device(): mine = lax.all_to_all(back, AXES, split_axis=0, concat_axis=0, tiled=True)  18 us
    pallas_call x1, Pallas kernels, on_device(): pl.pallas_call(functools.partial(client_kernel, shares=shares, chunk=chun...  10.2 us

profile of v4, /device:TPU:0, one launch (start us, length us, event | category | flops | bytes accessed | tf_op | source)
XLA Modules:
  0.0 54.3 jit_solution(16793115585968877144)
XLA Ops:
  1.3 10.2 %client.1 = f32[1056,128]{1,0:T(8,128)S(1)} custom-call(s32[1,2,1024]{2,1,0:T(2,128)} %rows_hbm.1, s32[1]{0:T(128)S(6)} %copy.10.count_ref, s32[1]{0:T(128)S(6)} %copy.11.cluster_ref, bf16[1,2048,1024]{2,1,0:T(8,128)(2,1)} %features_ref.1, bf16[1,1024,512]{2,1,0:T(8,128)(2,1)} %lower_ref.1, bf16[1,2048,256]{2,1,0:T(8,128)(2,1)} %targets_ref.1, ...), custom_call_target="tpu_custom_call" | custom-call | tf_op jit(solution)/shard_map/client/pallas_call | solution.py:186
  11.5 23.4 %all_to_all.10 = f32[1056,1,128]{2,1,0:T(1,128)S(1)} all-to-all(f32[1056,1,128]{2,1,0:T(1,128)S(1)} %bitcast.5), channel_id=1, replica_groups=mesh['chip'=2,'board'=4,'cuts'=4] {'chip','board','cuts'}, dimensions={0} | all-to-all | bytes 1081344 | tf_op jit(solution)/shard_map/all_to_all | solution.py:212
  34.8 0.7 %cluster.1 = f32[32,16,256]{2,1,0:T(8,128)S(1)} custom-call(f32[1056,128]{1,0:T(8,128)S(1)} %bitcast.6), custom_call_target="tpu_custom_call" | custom-call | tf_op jit(solution)/shard_map/cluster/pallas_call | solution.py:213
  35.5 18.0 %all_to_all.11 = f32[32,16,256]{2,1,0:T(8,128)S(1)} all-to-all(f32[32,16,256]{2,1,0:T(8,128)S(1)} %cluster.1), channel_id=1, replica_groups=mesh['chip'=2,'board'=4,'cuts'=4] {'chip','board','cuts'}, dimensions={0} | all-to-all | bytes 1048576 | tf_op jit(solution)/shard_map/all_to_all | solution.py:221
  53.5 0.8 %copy.12 = f32[1,512,256]{2,1,0:T(8,128)} copy(f32[1,512,256]{2,1,0:T(8,128)S(1)} %bitcast.7) | data formatting | bytes 1048576

commit v5 on v4

--- a/solution.py
+++ b/solution.py
@@ -33,7 +33,7 @@
     outs = targ.shape[1]
     blocks, tblocks = hidden // LANES, outs // LANES
     scale = -(LR / count_rows)
-    sizes = [chunk] * 2 + [2 * chunk] * ((pool_rows - 2 * chunk) // (2 * chunk))
+    sizes = [chunk // 2] * 2 + [chunk] * ((pool_rows - chunk) // chunk)
     sizes += [pool_rows - sum(sizes)] * (sum(sizes) < pool_rows)
     offsets = [sum(sizes[:i]) for i in range(len(sizes))]
 
@@ -174,7 +174,7 @@
     shares = lax.axis_size(AXES)
     pool_rows, inputs = features.shape[1:]
     hidden, outs = head_weight.shape[1:]
-    chunk = 256
+    chunk = 512
     each = hidden // shares
     tblocks = outs // LANES
     width = tblocks * each + 1
@@ -202,7 +202,7 @@
             pltpu.VMEM((outs, hidden), F32),
             pltpu.VMEM((outs, hidden), F32),
             pltpu.VMEM((2 * outs, hidden), BF16),
-            pltpu.SemaphoreType.DMA((pool_rows // chunk + 4 + steps,)),
+            pltpu.SemaphoreType.DMA((pool_rows // chunk + 8 + steps,)),
         ],
         compiler_params=pltpu.CompilerParams(vmem_limit_bytes=VMEM_LIMIT),
         name="client",

time: 54.5 us -> 54.3 us (level)
  no operation moved by 1% of the time
where the time goes in v5:
time: 54.3 us; the launch traced here: 54.1 us
  blocking collectives  41.4 us (76%)
  Pallas kernels  10.7 us (20%)
  between operations  1.31 us (2%)
  local copies, waits for them, and re-layouts  0.79 us (1%)
    all_to_all x1, blocking collectives, on_device(): lax.all_to_all(outgoing.reshape(shares * width, 1, LANES), AXES, split_ax...  23.4 us
    all_to_all x1, blocking collectives, on_device(): mine = lax.all_to_all(back, AXES, split_axis=0, concat_axis=0, tiled=True)  18 us
    pallas_call x1, Pallas kernels, on_device(): pl.pallas_call(functools.partial(client_kernel, shares=shares, chunk=chun...  9.99 us

profile of v5, /device:TPU:0, one launch (start us, length us, event | category | flops | bytes accessed | tf_op | source)
XLA Modules:
  0.0 54.1 jit_solution(8948580417365644273)
XLA Ops:
  1.3 10.0 %client.1 = f32[1056,128]{1,0:T(8,128)S(1)} custom-call(s32[1,2,1024]{2,1,0:T(2,128)} %rows_hbm.1, s32[1]{0:T(128)S(6)} %copy.10.count_ref, s32[1]{0:T(128)S(6)} %copy.11.cluster_ref, bf16[1,2048,1024]{2,1,0:T(8,128)(2,1)} %features_ref.1, bf16[1,1024,512]{2,1,0:T(8,128)(2,1)} %lower_ref.1, bf16[1,2048,256]{2,1,0:T(8,128)(2,1)} %targets_ref.1, ...), custom_call_target="tpu_custom_call" | custom-call | tf_op jit(solution)/shard_map/client/pallas_call | solution.py:186
  11.3 23.4 %all_to_all.10 = f32[1056,1,128]{2,1,0:T(1,128)S(1)} all-to-all(f32[1056,1,128]{2,1,0:T(1,128)S(1)} %bitcast.5), channel_id=1, replica_groups=mesh['chip'=2,'board'=4,'cuts'=4] {'chip','board','cuts'}, dimensions={0} | all-to-all | bytes 1081344 | tf_op jit(solution)/shard_map/all_to_all | solution.py:212
  34.7 0.7 %cluster.1 = f32[32,16,256]{2,1,0:T(8,128)S(1)} custom-call(f32[1056,128]{1,0:T(8,128)S(1)} %bitcast.6), custom_call_target="tpu_custom_call" | custom-call | tf_op jit(solution)/shard_map/cluster/pallas_call | solution.py:213
  35.4 18.0 %all_to_all.11 = f32[32,16,256]{2,1,0:T(8,128)S(1)} all-to-all(f32[32,16,256]{2,1,0:T(8,128)S(1)} %cluster.1), channel_id=1, replica_groups=mesh['chip'=2,'board'=4,'cuts'=4] {'chip','board','cuts'}, dimensions={0} | all-to-all | bytes 1048576 | tf_op jit(solution)/shard_map/all_to_all | solution.py:221
  53.3 0.8 %copy.12 = f32[1,512,256]{2,1,0:T(8,128)} copy(f32[1,512,256]{2,1,0:T(8,128)S(1)} %bitcast.7) | data formatting | bytes 1048576

commit v6 on v5

--- a/solution.py
+++ b/solution.py
@@ -128,7 +128,7 @@
             if step + 1 < steps:
                 load_weight(begin[...] + scale * total[...])
 
-    first[...] = total[...].T
+    delta = (total[...] * scale).T
 
     each = hidden // shares
     width = tblocks * each + 1
@@ -137,7 +137,7 @@
     for s in range(shares):
         for k in range(tblocks):
             out_ref[s * width + k * each:s * width + (k + 1) * each, :] = (
-                first[s * each:(s + 1) * each, k * LANES:(k + 1) * LANES] * scale
+                delta[s * each:(s + 1) * each, k * LANES:(k + 1) * LANES]
             )
         out_ref[(s + 1) * width - 1:(s + 1) * width, :] = note
 
@@ -161,7 +161,7 @@
             weight = jnp.where(ident == c, count, 0.0)
             counts[c] = counts[c] + weight
             sums[c] = sums[c] + weight * delta
-    sums = [total / (LR * count) for total, count in zip(sums, counts)]
+    sums = [total * (1.0 / (LR * count)) for total, count in zip(sums, counts)]
     for j in range(shares):
         mine = sums[0]
         for c in range(1, CLUSTERS):

time: 54.3 us -> 54.3 us (level)
  no operation moved by 1% of the time
where the time goes in v6:
time: 54.3 us; the launch traced here: 54.1 us
  blocking collectives  41.4 us (76%)
  Pallas kernels  10.7 us (20%)
  between operations  1.31 us (2%)
  local copies, waits for them, and re-layouts  0.79 us (1%)
    all_to_all x1, blocking collectives, on_device(): lax.all_to_all(outgoing.reshape(shares * width, 1, LANES), AXES, split_ax...  23.4 us
    all_to_all x1, blocking collectives, on_device(): mine = lax.all_to_all(back, AXES, split_axis=0, concat_axis=0, tiled=True)  18 us
    pallas_call x1, Pallas kernels, on_device(): pl.pallas_call(functools.partial(client_kernel, shares=shares, chunk=chun...  10 us

profile of v6, /device:TPU:0, one launch (start us, length us, event | category | flops | bytes accessed | tf_op | source)
XLA Modules:
  0.0 54.1 jit_solution(17650201495829386742)
XLA Ops:
  1.3 10.0 %client.1 = f32[1056,128]{1,0:T(8,128)S(1)} custom-call(s32[1,2,1024]{2,1,0:T(2,128)} %rows_hbm.1, s32[1]{0:T(128)S(6)} %copy.10.count_ref, s32[1]{0:T(128)S(6)} %copy.11.cluster_ref, bf16[1,2048,1024]{2,1,0:T(8,128)(2,1)} %features_ref.1, bf16[1,1024,512]{2,1,0:T(8,128)(2,1)} %lower_ref.1, bf16[1,2048,256]{2,1,0:T(8,128)(2,1)} %targets_ref.1, ...), custom_call_target="tpu_custom_call" | custom-call | tf_op jit(solution)/shard_map/client/pallas_call | solution.py:186
  11.3 23.4 %all_to_all.10 = f32[1056,1,128]{2,1,0:T(1,128)S(1)} all-to-all(f32[1056,1,128]{2,1,0:T(1,128)S(1)} %bitcast.5), channel_id=1, replica_groups=mesh['chip'=2,'board'=4,'cuts'=4] {'chip','board','cuts'}, dimensions={0} | all-to-all | bytes 1081344 | tf_op jit(solution)/shard_map/all_to_all | solution.py:212
  34.7 0.7 %cluster.1 = f32[32,16,256]{2,1,0:T(8,128)S(1)} custom-call(f32[1056,128]{1,0:T(8,128)S(1)} %bitcast.6), custom_call_target="tpu_custom_call" | custom-call | tf_op jit(solution)/shard_map/cluster/pallas_call | solution.py:213
  35.4 18.0 %all_to_all.11 = f32[32,16,256]{2,1,0:T(8,128)S(1)} all-to-all(f32[32,16,256]{2,1,0:T(8,128)S(1)} %cluster.1), channel_id=1, replica_groups=mesh['chip'=2,'board'=4,'cuts'=4] {'chip','board','cuts'}, dimensions={0} | all-to-all | bytes 1048576 | tf_op jit(solution)/shard_map/all_to_all | solution.py:221
  53.4 0.8 %copy.12 = f32[1,512,256]{2,1,0:T(8,128)} copy(f32[1,512,256]{2,1,0:T(8,128)S(1)} %bitcast.7) | data formatting | bytes 1048576
